TPU v7x, 32 devices: a whole 2x2x4 slice. The times are simulated.
32 devices in a mesh: group: 2 (over y), view: 4 (over z), depth: 2 (over x), row: 2 (over core).
Axes of the slice: x: 2, y: 2, z: 4, core: 2. Of those that a mesh axis runs over, the one named last changes fastest.
Arguments:
- features: float32 [4, 32, 8, 512], P('view', None, ('group', 'row')), parts along dimension 2, may hold values from -6 to 6
- cotangent: float32 [8, 32, 8, 512], P('depth', 'view', ('group', 'row')), parts along dimension 2, may hold values from -6 to 6
- src_row: int32 [4, 8, 8, 512], P('view', 'depth', ('group', 'row')), parts along dimension 2, may hold values from -2 to 4, as said below
- src_col: int32 [4, 8, 8, 512], P('view', 'depth', ('group', 'row')), parts along dimension 2, may hold values from 0 to 510
- fractions: int32 [2, 4, 8, 8, 512], P(None, 'view', 'depth', ('group', 'row')), parts along dimension 3, may hold values from 0 to 256
Outputs:
- grad_features: float32 [4, 32, 8, 512], P('view', None, ('group', 'row'), 'depth'), parts along dimension 2
There are 2 independent parts, one for each index of `group`. A program takes and returns all parts, laid end to end along the dimension named above; each array names one. Nothing has to cross between parts.
Inputs may be any that keep to these rules, and one draw needn't show every extreme that they name: src_row[v, d, y, x] lies between y - 2 and y + 1.
All inputs are finite; a program needn't handle non-finite values.
Results may differ from a plain program's by a relative error of at most 0.0003.
Values sent between devices are 32-bit elements; how exact they have to be, the bound alone decides.
A program may use at most 64 MiB of HBM per device.

v0:
```python
import functools

import jax
import jax.numpy as jnp
from jax import lax
from jax.experimental import pallas as pl
from jax.experimental.pallas import tpu as pltpu
from jax.sharding import PartitionSpec as P

MESH = pl.DeviceIdType.MESH
F32 = jnp.float32
BF16 = jnp.bfloat16
TILE = 256
CHUNK = 64
KEEP_BYTES = 24 << 20


def split(value):
    high = value.astype(BF16)
    low = (value - high.astype(F32)).astype(BF16)
    return jnp.concatenate([high, low], axis=0)


def kernel(
    sizes, feat, cot, srow, scol, frac, out,
    fown, fbuf, rbuf, cbuf, wbuf, cotv, lane_q, stack, mats, warp, wsum, cotg, outbuf, pbuf, red, inbuf,
    local_sem, f_send, f_recv, p_send, p_recv, i_send, i_recv, d_send, d_recv, o_send, o_recv,
):
    views, depths, rows, cc, planes, rl, width, keep = sizes
    me = lax.axis_index("view")
    mx = lax.axis_index("depth")
    mr = lax.axis_index("row")
    height = rows * rl
    wx = width // depths
    factor = 2.0 / views

    def view_at(step):
        return lax.rem(me + step, views)

    def row_at(step):
        return lax.rem(mr + step, rows)

    def depth_at(step):
        return lax.rem(mx + step, depths)

    barrier = pltpu.get_barrier_semaphore()

    def greet(v, x, r):
        pl.semaphore_signal(
            barrier, inc=1, device_id={"view": v, "depth": x, "row": r}, device_id_type=MESH
        )

    @pl.loop(1, views)
    def _(step):
        for dx in range(depths):
            greet(view_at(step), depth_at(dx), mr)

    for dx in range(1, depths):
        greet(me, depth_at(dx), mr)
    for dr in range(1, rows):
        greet(me, mx, row_at(dr))

    local = [
        pltpu.make_async_copy(feat.at[0], fown, local_sem.at[0]),
        pltpu.make_async_copy(feat.at[0, pl.ds(me * cc, cc)], fbuf.at[me, mr], local_sem.at[1]),
        pltpu.make_async_copy(srow.at[0], rbuf.at[me], local_sem.at[2]),
        pltpu.make_async_copy(scol.at[0], cbuf.at[me], local_sem.at[3]),
        pltpu.make_async_copy(frac.at[:, 0], wbuf.at[me], local_sem.at[4]),
        pltpu.make_async_copy(cot, cotv, local_sem.at[5]),
    ]
    for copy in local:
        copy.start()
    for j in range(TILE // CHUNK):
        part = lax.broadcasted_iota(jnp.int32, (CHUNK, width), 0) + j * CHUNK
        lane_q[pl.ds(j * CHUNK, CHUNK), :] = part.astype(F32).astype(BF16)
    row_of = (lax.broadcasted_iota(jnp.int32, (height * cc, width), 0) // cc).astype(F32)

    def feat_copy(step):
        to = lax.rem(me + views - step, views)
        return pltpu.make_async_remote_copy(
            src_ref=fown.at[pl.ds(to * cc, cc)], dst_ref=fbuf.at[me, mr],
            send_sem=f_send.at[step], recv_sem=f_recv.at[step],
            device_id={"view": to}, device_id_type=MESH,
        )

    def pass_copy(step, dr):
        block = fbuf.at[view_at(step), mr]
        return pltpu.make_async_remote_copy(
            src_ref=block, dst_ref=block,
            send_sem=p_send.at[step, dr], recv_sem=p_recv.at[step, dr],
            device_id={"row": row_at(dr)}, device_id_type=MESH,
        )

    def index_copies(step):
        to = lax.rem(me + views - step, views)
        return [
            pltpu.make_async_remote_copy(
                src_ref=block.at[me], dst_ref=block.at[me],
                send_sem=i_send.at[step, at], recv_sem=i_recv.at[step, at],
                device_id={"view": to}, device_id_type=MESH,
            )
            for at, block in enumerate((rbuf, cbuf, wbuf))
        ]

    def build(slot, v, d, i):
        col = cbuf[v, d, pl.ds(i, 1), :].astype(F32)
        fx = (wbuf[v, 1, d, pl.ds(i, 1), :].astype(F32) / 256.0).astype(BF16)
        fx = jnp.broadcast_to(fx, (CHUNK, width))
        for t in range(width // TILE):
            c = jnp.broadcast_to((col - float(t * TILE)).astype(BF16), (CHUNK, width))
            for j in range(TILE // CHUNK):
                apart = (lane_q[pl.ds(j * CHUNK, CHUNK), :] - c) - fx
                mats[slot, pl.ds(t * TILE + j * CHUNK, CHUNK), :] = jnp.maximum(
                    BF16(1.0) - jnp.abs(apart), BF16(0.0)
                )

    def slot_of(v, d, i):
        at = d * rl + i
        return v * (planes * rl) + at if keep else at

    def row_weight(v, d, i):
        row = rbuf[v, d, pl.ds(i, 1), :].astype(F32)
        fy = wbuf[v, 0, d, pl.ds(i, 1), :].astype(F32) / 256.0
        return jnp.maximum(1.0 - jnp.abs(row_of - (row + fy)), 0.0)

    def build_all(v):
        for d in range(planes):
            for i in range(rl):
                build(slot_of(v, d, i), v, d, i)

    def sampled(v, first):
        for s in range(rows):
            for i in range(rl):
                stack[pl.ds((s * rl + i) * cc, cc), :] = fbuf[v, s, :, i, :]
        both_parts = split(stack[...])
        for d in range(planes):
            for i in range(rl):
                if not first:
                    build(slot_of(v, d, i), v, d, i)
                both = jnp.dot(both_parts, mats[slot_of(v, d, i)], preferred_element_type=F32)
                mixed = (both[: height * cc] + both[height * cc :]) * row_weight(v, d, i)
                warped = mixed[:cc]
                for h in range(1, height):
                    warped = warped + mixed[h * cc : (h + 1) * cc]
                warp[v, d, i] = warped
                wsum[d, i] = warped if first else wsum[d, i] + warped

    for copy in local[2:5]:
        copy.wait()
    build_all(me)
    for copy in local[:2]:
        copy.wait()
    pl.semaphore_wait(barrier, views * depths + rows - 2)

    for dr in range(1, rows):
        pass_copy(0, dr).start()

    @pl.loop(1, views)
    def _(step):
        feat_copy(step).start()

    @pl.loop(1, views)
    def _(step):
        for copy in index_copies(step):
            copy.start()

    local[5].wait()
    for d in range(planes):
        for i in range(rl):
            cotg[d, i] = factor * cotv[d, :, i, :]
    for dr in range(1, rows):
        pass_copy(0, dr).wait_recv()
    sampled(me, True)

    @pl.loop(1, views)
    def _(step):
        feat_copy(step).wait_recv()
        for dr in range(1, rows):
            pass_copy(step, dr).start()

    @pl.loop(1, views)
    def _(step):
        for copy in index_copies(step):
            copy.wait_recv()
        for dr in range(1, rows):
            pass_copy(step, dr).wait_recv()
        sampled(view_at(step), False)

    def backward(v):
        if not keep:
            build_all(v)
        both = None
        for d in range(planes):
            for i in range(rl):
                grad = cotg[d, i] * (warp[v, d, i] - wsum[d, i] / views)
                moved = jnp.concatenate([grad] * height, axis=0) * row_weight(v, d, i)
                term = lax.dot_general(
                    split(moved), mats[slot_of(v, d, i)], (((1,), (1,)), ((), ())),
                    preferred_element_type=F32,
                )
                both = term if both is None else both + term
        total = both[: height * cc] + both[height * cc :]
        for s in range(rows):
            for x in range(depths):
                for i in range(rl):
                    at = (s * rl + i) * cc
                    outbuf[v, s, x, i] = total[at : at + cc, x * wx : (x + 1) * wx]

    def core_copy(v, dr):
        r = row_at(dr)
        return pltpu.make_async_remote_copy(
            src_ref=outbuf.at[v, r], dst_ref=pbuf.at[v, dr],
            send_sem=d_send.at[v, dr], recv_sem=d_recv.at[v, dr],
            device_id={"row": r}, device_id_type=MESH,
        )

    def out_copy(v, step, dx):
        x = depth_at(dx)
        return pltpu.make_async_remote_copy(
            src_ref=red.at[v, x], dst_ref=inbuf.at[me, mx],
            send_sem=o_send.at[step, dx], recv_sem=o_recv.at[step, dx],
            device_id={"view": v, "depth": x}, device_id_type=MESH,
        )

    def start_core(v):
        for dr in range(1, rows):
            core_copy(v, dr).start()

    def add_cores(v, target, x):
        piece = outbuf[v, mr, x]
        for dr in range(1, rows):
            piece = piece + pbuf[v, dr, x]
        target[...] = piece

    def pass_on(step):
        v = view_at(step)
        for dr in range(1, rows):
            core_copy(v, dr).wait_recv()
        for x in range(depths):
            add_cores(v, red.at[v, x], x)
        for dx in range(depths):
            out_copy(v, step, dx).start()

    @pl.loop(1, views)
    def _(step):
        v = view_at(step)
        backward(v)
        start_core(v)

        @pl.when(step > 1)
        def _():
            pass_on(step - 1)

    backward(me)
    start_core(me)
    if views > 1:
        pass_on(views - 1)
    for dr in range(1, rows):
        core_copy(me, dr).wait_recv()
    for dx in range(1, depths):
        add_cores(me, red.at[me, depth_at(dx)], depth_at(dx))
        out_copy(me, 0, dx).start()
    add_cores(me, inbuf.at[me, mx], mx)

    @pl.loop(1, views)
    def _(step):
        for dx in range(depths):
            out_copy(view_at(step), step, dx).wait_recv()

    for dx in range(1, depths):
        out_copy(me, 0, dx).wait_recv()

    for i in range(rl):
        for u in range(views):
            piece = inbuf[u, 0, i]
            for x in range(1, depths):
                piece = piece + inbuf[u, x, i]
            out[i, pl.ds(u * cc, cc), :] = piece

    for dr in range(1, rows):
        pass_copy(0, dr).wait_send()
        core_copy(me, dr).wait_send()
    for dx in range(1, depths):
        out_copy(me, 0, dx).wait_send()

    @pl.loop(1, views)
    def _(step):
        feat_copy(step).wait_send()
        for copy in index_copies(step):
            copy.wait_send()
        for dr in range(1, rows):
            pass_copy(step, dr).wait_send()
            core_copy(view_at(step), dr).wait_send()
        for dx in range(depths):
            out_copy(view_at(step), step, dx).wait_send()


def per_device(features, cotangent, src_row, src_col, fractions):
    views, depths, rows = (lax.axis_size(axis) for axis in ("view", "depth", "row"))
    channels, rl, width = features.shape[1:]
    planes, cc = cotangent.shape[:2]
    height, wx = rows * rl, width // depths
    matrices = views * planes * rl
    keep = matrices * width * width * 2 <= KEEP_BYTES
    sizes = (views, depths, rows, cc, planes, rl, width, keep)
    grad = pl.pallas_call(
        functools.partial(kernel, sizes),
        out_shape=jax.ShapeDtypeStruct((rl, channels, wx), F32),
        in_specs=[pl.BlockSpec(memory_space=pl.ANY)] * 5,
        out_specs=pl.BlockSpec(memory_space=pltpu.VMEM),
        scratch_shapes=[
            pltpu.VMEM((channels, rl, width), F32),
            pltpu.VMEM((views, rows, cc, rl, width), F32),
            pltpu.VMEM((views, planes, rl, width), jnp.int32),
            pltpu.VMEM((views, planes, rl, width), jnp.int32),
            pltpu.VMEM((views, 2, planes, rl, width), jnp.int32),
            pltpu.VMEM((planes, cc, rl, width), F32),
            pltpu.VMEM((TILE, width), BF16),
            pltpu.VMEM((height * cc, width), F32),
            pltpu.VMEM((matrices if keep else planes * rl, width, width), BF16),
            pltpu.VMEM((views, planes, rl, cc, width), F32),
            pltpu.VMEM((planes, rl, cc, width), F32),
            pltpu.VMEM((planes, rl, cc, width), F32),
            pltpu.VMEM((views, rows, depths, rl, cc, wx), F32),
            pltpu.VMEM((views, rows, depths, rl, cc, wx), F32),
            pltpu.VMEM((views, depths, rl, cc, wx), F32),
            pltpu.VMEM((views, depths, rl, cc, wx), F32),
            pltpu.SemaphoreType.DMA((6,)),
            pltpu.SemaphoreType.DMA((views,)),
            pltpu.SemaphoreType.DMA((views,)),
            pltpu.SemaphoreType.DMA((views, rows)),
            pltpu.SemaphoreType.DMA((views, rows)),
            pltpu.SemaphoreType.DMA((views, 3)),
            pltpu.SemaphoreType.DMA((views, 3)),
            pltpu.SemaphoreType.DMA((views, rows)),
            pltpu.SemaphoreType.DMA((views, rows)),
            pltpu.SemaphoreType.DMA((views, depths)),
            pltpu.SemaphoreType.DMA((views, depths)),
        ],
        compiler_params=pltpu.CompilerParams(
            collective_id=0, has_side_effects=True, vmem_limit_bytes=56 << 20
        ),
    )(features, cotangent, src_row, src_col, fractions)
    return jnp.transpose(grad, (1, 0, 2))[None]


def solution(mesh):
    in_specs = (
        P("view", None, ("group", "row"), None),
        P("depth", "view", ("group", "row"), None),
        P("view", "depth", ("group", "row"), None),
        P("view", "depth", ("group", "row"), None),
        P(None, "view", "depth", ("group", "row"), None),
    )
    out_specs = P("view", None, ("group", "row"), "depth")
    return jax.shard_map(
        per_device, mesh=mesh, in_specs=in_specs, out_specs=out_specs, check_vma=False
    )
```

profile of v0, /device:TPU:0, one launch (start us, length us, event | category | flops | bytes accessed | tf_op | source)
XLA Modules:
  0.0 30.1 jit_solution(2255722086935811623)
XLA Ops:
  0.0 28.5 %shard_map.55 = f32[2,32,256]{2,1,0:T(8,128)} custom-call(f32[1,32,2,512]{3,2,1,0:T(2,128)} %feat.1, f32[4,8,2,512]{3,2,1,0:T(2,128)} %cot.1, s32[1,4,2,512]{3,2,1,0:T(2,128)} %srow.1, s32[1,4,2,512]{3,2,1,0:T(2,128)} %scol.1, s32[2,1,4,2,512]{4,3,2,1,0:T(2,128)} %frac.1), custom_call_target="tpu_custom_call" | custom-call | tf_op jit(solution)/shard_map/pallas_call | solution.py:306
  28.5 1.5 %copy.6 = f32[1,32,2,256]{3,2,1,0:T(2,128)} copy(f32[1,32,2,256]{3,1,2,0:T(8,128)} %bitcast.3) | data formatting | bytes 131072 | tf_op jit(solution)/shard_map/broadcast_in_dim | solution.py:344
where the time goes:
time: 30.2 us; the launch traced here: 30.1 us
  Pallas kernels  28.5 us (94%)
  local copies, waits for them, and re-layouts  1.52 us (5%)
    pallas_call x1, Pallas kernels, per_device(): pl.pallas_call(functools.partial(kernel, sizes), out_shape=jax.ShapeDtype...  28.5 us
    broadcast_in_dim x1, local copies, waits for them, and re-layouts, per_device(): return jnp.transpose(grad, (1, 0, 2))[None]  1.52 us

commit v1 on v0

v1 whole, which is shorter than its diff:
```python
import functools

import jax
import jax.numpy as jnp
from jax import lax
from jax.experimental import pallas as pl
from jax.experimental.pallas import tpu as pltpu
from jax.sharding import PartitionSpec as P

MESH = pl.DeviceIdType.MESH
F32 = jnp.float32
BF16 = jnp.bfloat16
SPAN = 128
STRIDE = SPAN - 1
COLS = 256
UNROLL = 4


def split(value, axis):
    high = value.astype(BF16)
    low = (value - high.astype(F32)).astype(BF16)
    return jnp.concatenate([high, low], axis=axis)


def kernel(
    sizes, feat, cot, srow, scol, frac, out,
    fbuf, sbuf, qbuf, wbuf, cbuf, cotv, cotg, flat, mats, moved, warp, wsum, outbuf, pbuf, red, inbuf,
    local_sem, f_send, f_recv, p_send, p_recv, i_send, i_recv, d_send, d_recv, o_send, o_recv,
):
    views, depths, rows, cc, planes, rl, width = sizes
    me = lax.axis_index("view")
    mx = lax.axis_index("depth")
    mr = lax.axis_index("row")
    height = rows * rl
    wx = width // depths
    lines = planes * rl
    spans = (width - 1) // STRIDE + 1
    factor = 2.0 / views
    siblings = [(dx, dr) for dx in range(depths) for dr in range(rows) if dx or dr]

    def view_at(step):
        return lax.rem(me + step, views)

    def row_at(step):
        return lax.rem(mr + step, rows)

    def depth_at(step):
        return lax.rem(mx + step, depths)

    def over_views(first, body):
        if views <= UNROLL:
            for step in range(first, views):
                body(step)
        else:
            pl.loop(first, views)(body)

    barrier = pltpu.get_barrier_semaphore()

    def greet(v, x, r):
        pl.semaphore_signal(
            barrier, inc=1, device_id={"view": v, "depth": x, "row": r}, device_id_type=MESH
        )

    over_views(1, lambda step: greet(view_at(step), mx, mr))
    for dx, dr in siblings:
        greet(me, depth_at(dx), row_at(dr))

    local = [
        pltpu.make_async_copy(srow.at[0], sbuf, local_sem.at[0]),
        pltpu.make_async_copy(scol.at[0], qbuf, local_sem.at[1]),
        pltpu.make_async_copy(frac.at[:, 0], wbuf, local_sem.at[2]),
        pltpu.make_async_copy(feat.at[0, pl.ds(me * cc, cc)], fbuf.at[me, mr], local_sem.at[3]),
        pltpu.make_async_copy(cot, cotv, local_sem.at[4]),
    ]
    for copy in local:
        copy.start()

    def feat_copy(step):
        to = lax.rem(me + views - step, views)
        return pltpu.make_async_remote_copy(
            src_ref=feat.at[0, pl.ds(to * cc, cc)], dst_ref=fbuf.at[me, mr],
            send_sem=f_send.at[step], recv_sem=f_recv.at[step],
            device_id={"view": to}, device_id_type=MESH,
        )

    def own_copy(dr):
        return pltpu.make_async_remote_copy(
            src_ref=feat.at[0, pl.ds(me * cc, cc)], dst_ref=fbuf.at[me, mr],
            send_sem=p_send.at[0, dr], recv_sem=p_recv.at[0, dr],
            device_id={"row": row_at(dr)}, device_id_type=MESH,
        )

    def pass_copy(step, dr):
        block = fbuf.at[view_at(step), mr]
        return pltpu.make_async_remote_copy(
            src_ref=block, dst_ref=block,
            send_sem=p_send.at[step, dr], recv_sem=p_recv.at[step, dr],
            device_id={"row": row_at(dr)}, device_id_type=MESH,
        )

    def point_copy(step):
        to = lax.rem(me + views - step, views)
        return pltpu.make_async_remote_copy(
            src_ref=cbuf.at[me], dst_ref=cbuf.at[me],
            send_sem=i_send.at[step], recv_sem=i_recv.at[step],
            device_id={"view": to}, device_id_type=MESH,
        )

    for copy in local[:3]:
        copy.wait()
    for d in range(planes):
        at = pl.ds(d * rl, rl)
        cbuf[me, 0, at, :] = sbuf[d].astype(F32) + wbuf[0, d].astype(F32) / 256.0
        cbuf[me, 1, at, :] = qbuf[d].astype(F32) + wbuf[1, d].astype(F32) / 256.0

    pl.semaphore_wait(barrier, views + len(siblings) - 1)
    for dr in range(1, rows):
        own_copy(dr).start()
    over_views(1, lambda step: feat_copy(step).start())
    over_views(1, lambda step: point_copy(step).start())

    lane = lax.broadcasted_iota(jnp.int32, (SPAN, COLS), 0).astype(F32).astype(BF16)

    def points(v):
        position = cbuf[v, 1]
        span = jnp.zeros_like(position)
        for t in range(1, spans):
            span = span + jnp.where(position >= float(t * STRIDE), 1.0, 0.0)
        inside = position - span * float(STRIDE)
        whole = jnp.floor(inside)
        return cbuf[v, 0], span, whole, inside - whole

    def row_weight(row, k, h):
        return jnp.maximum(1.0 - jnp.abs(row[k : k + 1] - float(h)), 0.0)

    def flatten(v):
        parts = []
        for h in range(height):
            line = fbuf[v, h // rl, :, h % rl, :]
            line = jnp.concatenate(
                [line, jnp.zeros((cc, (spans - 1) * STRIDE + SPAN - width), F32)], axis=1
            )
            for t in range(spans):
                parts.append(line[:, t * STRIDE : t * STRIDE + SPAN])
        flat[...] = split(jnp.concatenate(parts, axis=0), 1)

    def sampled(v, first):
        flatten(v)
        row, span, whole, rest = points(v)
        for k in range(lines):
            for n in range(0, width, COLS):
                cols = slice(n, n + COLS)
                at = jnp.broadcast_to(whole[k : k + 1, cols].astype(BF16), (SPAN, COLS))
                past = jnp.broadcast_to(rest[k : k + 1, cols].astype(BF16), (SPAN, COLS))
                mat = jnp.maximum(BF16(1.0) - jnp.abs((lane - at) - past), BF16(0.0))
                mats[v, :, k * width + n : k * width + n + COLS] = mat
                mixed = jnp.dot(
                    flat[...], jnp.concatenate([mat, mat], axis=0), preferred_element_type=F32
                )
                which = jnp.broadcast_to(span[k : k + 1, cols], (cc, COLS))
                warped = None
                for h in range(height):
                    base = h * spans * cc
                    part = mixed[base : base + cc]
                    for t in range(1, spans):
                        here = base + t * cc
                        part = jnp.where(which == float(t), mixed[here : here + cc], part)
                    part = part * row_weight(row, k, h)[:, cols]
                    warped = part if warped is None else warped + part
                warp[v, k, :, cols] = warped
                wsum[k, :, cols] = warped if first else wsum[k, :, cols] + warped

    local[4].wait()
    for k in range(lines):
        cotg[k] = factor * cotv[k // rl, :, k % rl, :]
    local[3].wait()
    for dr in range(1, rows):
        own_copy(dr).wait_recv()
    sampled(me, True)

    def pass_features(step):
        feat_copy(step).wait_recv()
        for dr in range(1, rows):
            pass_copy(step, dr).start()

    over_views(1, pass_features)

    def sample_step(step):
        point_copy(step).wait_recv()
        for dr in range(1, rows):
            pass_copy(step, dr).wait_recv()
        sampled(view_at(step), False)

    over_views(1, sample_step)

    def backward(v):
        row, span, _, _ = points(v)
        for k in range(lines):
            grad = cotg[k] * (warp[v, k] - wsum[k] / views)
            both = split(
                jnp.concatenate([grad * row_weight(row, k, h) for h in range(height)], axis=0), 0
            )
            size = 2 * height * cc
            for t in range(spans):
                mask = jnp.where(span[k : k + 1] == float(t), 1.0, 0.0).astype(BF16)
                moved[t * size : (t + 1) * size, k * width : (k + 1) * width] = both * mask
        total = lax.dot_general(
            moved[...], mats[v], (((1,), (1,)), ((), ())), preferred_element_type=F32
        )
        whole = None
        for t in range(spans):
            left = t * STRIDE
            part = total[t * size : t * size + size // 2] + total[t * size + size // 2 : (t + 1) * size]
            part = part[:, : min(SPAN, width - left)]
            right = width - left - part.shape[1]
            pieces = [jnp.zeros((size // 2, left), F32)] if left else []
            pieces.append(part)
            if right:
                pieces.append(jnp.zeros((size // 2, right), F32))
            part = jnp.concatenate(pieces, axis=1)
            whole = part if whole is None else whole + part
        for s in range(rows):
            for x in range(depths):
                for i in range(rl):
                    at = (s * rl + i) * cc
                    outbuf[v, s, x, i] = whole[at : at + cc, x * wx : (x + 1) * wx]

    def piece_copy(v, dx, dr):
        x, r = depth_at(dx), row_at(dr)
        at = dx * rows + dr
        return pltpu.make_async_remote_copy(
            src_ref=outbuf.at[v, r, x], dst_ref=pbuf.at[v, at],
            send_sem=d_send.at[v, at], recv_sem=d_recv.at[v, at],
            device_id={"depth": x, "row": r}, device_id_type=MESH,
        )

    def out_copy(step):
        v = view_at(step)
        return pltpu.make_async_remote_copy(
            src_ref=red.at[v], dst_ref=inbuf.at[me],
            send_sem=o_send.at[step], recv_sem=o_recv.at[step],
            device_id={"view": v}, device_id_type=MESH,
        )

    def add_pieces(v, target):
        piece = outbuf[v, mr, mx]
        for dx, dr in siblings:
            piece_copy(v, dx, dr).wait_recv()
            piece = piece + pbuf[v, dx * rows + dr]
        target[...] = piece

    def pass_on(step):
        v = view_at(step)
        add_pieces(v, red.at[v])
        out_copy(step).start()

    def backward_step(step):
        v = view_at(step)
        backward(v)
        for dx, dr in siblings:
            piece_copy(v, dx, dr).start()
        if views <= UNROLL:
            if step > 1:
                pass_on(step - 1)
        else:
            @pl.when(step > 1)
            def _():
                pass_on(step - 1)

    over_views(1, backward_step)
    backward(me)
    for dx, dr in siblings:
        piece_copy(me, dx, dr).start()
    if views > 1:
        pass_on(views - 1)
    add_pieces(me, inbuf.at[me])

    over_views(1, lambda step: out_copy(step).wait_recv())
    for i in range(rl):
        for u in range(views):
            out[i, pl.ds(u * cc, cc), :] = inbuf[u, i]

    for dr in range(1, rows):
        own_copy(dr).wait_send()
    for dx, dr in siblings:
        piece_copy(me, dx, dr).wait_send()

    def finish(step):
        feat_copy(step).wait_send()
        point_copy(step).wait_send()
        for dr in range(1, rows):
            pass_copy(step, dr).wait_send()
        for dx, dr in siblings:
            piece_copy(view_at(step), dx, dr).wait_send()
        out_copy(step).wait_send()

    over_views(1, finish)


def per_device(features, cotangent, src_row, src_col, fractions):
    views, depths, rows = (lax.axis_size(axis) for axis in ("view", "depth", "row"))
    channels, rl, width = features.shape[1:]
    planes, cc = cotangent.shape[:2]
    height, wx = rows * rl, width // depths
    lines = planes * rl
    spans = (width - 1) // STRIDE + 1
    sizes = (views, depths, rows, cc, planes, rl, width)
    grad = pl.pallas_call(
        functools.partial(kernel, sizes),
        out_shape=jax.ShapeDtypeStruct((rl, channels, wx), F32),
        in_specs=[pl.BlockSpec(memory_space=pl.ANY)] * 5,
        out_specs=pl.BlockSpec(memory_space=pltpu.VMEM),
        scratch_shapes=[
            pltpu.VMEM((views, rows, cc, rl, width), F32),
            pltpu.VMEM((planes, rl, width), jnp.int32),
            pltpu.VMEM((planes, rl, width), jnp.int32),
            pltpu.VMEM((2, planes, rl, width), jnp.int32),
            pltpu.VMEM((views, 2, lines, width), F32),
            pltpu.VMEM((planes, cc, rl, width), F32),
            pltpu.VMEM((lines, cc, width), F32),
            pltpu.VMEM((height * spans * cc, 2 * SPAN), BF16),
            pltpu.VMEM((views, SPAN, lines * width), BF16),
            pltpu.VMEM((2 * height * spans * cc, lines * width), BF16),
            pltpu.VMEM((views, lines, cc, width), F32),
            pltpu.VMEM((lines, cc, width), F32),
            pltpu.VMEM((views, rows, depths, rl, cc, wx), F32),
            pltpu.VMEM((views, rows * depths, rl, cc, wx), F32),
            pltpu.VMEM((views, rl, cc, wx), F32),
            pltpu.VMEM((views, rl, cc, wx), F32),
            pltpu.SemaphoreType.DMA((5,)),
            pltpu.SemaphoreType.DMA((views,)),
            pltpu.SemaphoreType.DMA((views,)),
            pltpu.SemaphoreType.DMA((views, rows)),
            pltpu.SemaphoreType.DMA((views, rows)),
            pltpu.SemaphoreType.DMA((views,)),
            pltpu.SemaphoreType.DMA((views,)),
            pltpu.SemaphoreType.DMA((views, rows * depths)),
            pltpu.SemaphoreType.DMA((views, rows * depths)),
            pltpu.SemaphoreType.DMA((views,)),
            pltpu.SemaphoreType.DMA((views,)),
        ],
        compiler_params=pltpu.CompilerParams(
            collective_id=0, has_side_effects=True, vmem_limit_bytes=60 << 20
        ),
    )(features, cotangent, src_row, src_col, fractions)
    return jnp.transpose(grad, (1, 0, 2))[None]


def solution(mesh):
    in_specs = (
        P("view", None, ("group", "row"), None),
        P("depth", "view", ("group", "row"), None),
        P("view", "depth", ("group", "row"), None),
        P("view", "depth", ("group", "row"), None),
        P(None, "view", "depth", ("group", "row"), None),
    )
    out_specs = P("view", None, ("group", "row"), "depth")
    return jax.shard_map(
        per_device, mesh=mesh, in_specs=in_specs, out_specs=out_specs, check_vma=False
    )
```

time: 30.2 us -> 27.8 us (0.921)
  Pallas kernels: 28.5 us -> 26 us
    pallas_call x1, Pallas kernels: 28.5 us -> 26 us  [per_device(): pl.pallas_call(functools.partial(kernel, sizes), out_shape=jax.ShapeDtype...]
where the time goes in v1:
time: 27.8 us; the launch traced here: 27.5 us
  Pallas kernels  26 us (94%)
  local copies, waits for them, and re-layouts  1.52 us (5%)
    pallas_call x1, Pallas kernels, per_device(): pl.pallas_call(functools.partial(kernel, sizes), out_shape=jax.ShapeDtype...  26 us
    broadcast_in_dim x1, local copies, waits for them, and re-layouts, per_device(): return jnp.transpose(grad, (1, 0, 2))[None]  1.52 us

profile of v1, /device:TPU:0, one launch (start us, length us, event | category | flops | bytes accessed | tf_op | source)
XLA Modules:
  0.0 27.5 jit_solution(15025312607871258386)
XLA Ops:
  0.0 26.0 %shard_map.55 = f32[2,32,256]{2,1,0:T(8,128)} custom-call(f32[1,32,2,512]{3,2,1,0:T(2,128)} %feat.1, f32[4,8,2,512]{3,2,1,0:T(2,128)} %cot.1, s32[1,4,2,512]{3,2,1,0:T(2,128)} %srow.1, s32[1,4,2,512]{3,2,1,0:T(2,128)} %scol.1, s32[2,1,4,2,512]{4,3,2,1,0:T(2,128)} %frac.1), custom_call_target="tpu_custom_call" | custom-call | tf_op jit(solution)/shard_map/pallas_call | solution.py:308
  26.0 1.5 %copy.6 = f32[1,32,2,256]{3,2,1,0:T(2,128)} copy(f32[1,32,2,256]{3,1,2,0:T(8,128)} %bitcast.3) | data formatting | bytes 131072 | tf_op jit(solution)/shard_map/broadcast_in_dim | solution.py:346

commit v2 on v1

--- a/solution.py
+++ b/solution.py
@@ -24,7 +24,7 @@
 
 def kernel(
     sizes, feat, cot, srow, scol, frac, out,
-    fbuf, sbuf, qbuf, wbuf, cbuf, cotv, cotg, flat, mats, moved, warp, wsum, outbuf, pbuf, red, inbuf,
+    fbuf, sbuf, qbuf, wbuf, cbuf, cotv, cotg, flat, mats, moved, warp, wsum, outbuf, pbuf, red,
     local_sem, f_send, f_recv, p_send, p_recv, i_send, i_recv, d_send, d_recv, o_send, o_recv,
 ):
     views, depths, rows, cc, planes, rl, width = sizes
@@ -38,21 +38,27 @@
     factor = 2.0 / views
     siblings = [(dx, dr) for dx in range(depths) for dr in range(rows) if dx or dr]
 
-    def view_at(step):
-        return lax.rem(me + step, views)
-
     def row_at(step):
         return lax.rem(mr + step, rows)
 
     def depth_at(step):
         return lax.rem(mx + step, depths)
 
-    def over_views(first, body):
+    def others(body):
         if views <= UNROLL:
-            for step in range(first, views):
-                body(step)
+            for at in range(1, views):
+                body(views - at)
         else:
-            pl.loop(first, views)(body)
+            pl.loop(1, views)(lambda at: body(views - at))
+
+    def paired(step):
+        if views & (views - 1):
+            return lax.rem(views - me + step, views)
+        other, bit = 0, 1
+        while bit < views:
+            other = other + bit * lax.rem(me // bit + step // bit, 2)
+            bit *= 2
+        return other
 
     barrier = pltpu.get_barrier_semaphore()
 
@@ -61,7 +67,7 @@
             barrier, inc=1, device_id={"view": v, "depth": x, "row": r}, device_id_type=MESH
         )
 
-    over_views(1, lambda step: greet(view_at(step), mx, mr))
+    others(lambda step: greet(paired(step), mx, mr))
     for dx, dr in siblings:
         greet(me, depth_at(dx), row_at(dr))
 
@@ -75,10 +81,12 @@
     for copy in local:
         copy.start()
 
+    mine = pl.ds(pl.multiple_of(mx * wx, SPAN), wx)
+
     def feat_copy(step):
-        to = lax.rem(me + views - step, views)
-        return pltpu.make_async_remote_copy(
-            src_ref=feat.at[0, pl.ds(to * cc, cc)], dst_ref=fbuf.at[me, mr],
+        to = paired(step)
+        return pltpu.make_async_remote_copy(
+            src_ref=feat.at[0, pl.ds(to * cc, cc), :, mine], dst_ref=fbuf.at[me, mr, :, :, mine],
             send_sem=f_send.at[step], recv_sem=f_recv.at[step],
             device_id={"view": to}, device_id_type=MESH,
         )
@@ -90,21 +98,28 @@
             device_id={"row": row_at(dr)}, device_id_type=MESH,
         )
 
-    def pass_copy(step, dr):
-        block = fbuf.at[view_at(step), mr]
-        return pltpu.make_async_remote_copy(
-            src_ref=block, dst_ref=block,
-            send_sem=p_send.at[step, dr], recv_sem=p_recv.at[step, dr],
-            device_id={"row": row_at(dr)}, device_id_type=MESH,
-        )
+    def pass_copies(step):
+        block = fbuf.at[paired(step), mr, :, :, mine]
+        return [
+            pltpu.make_async_remote_copy(
+                src_ref=block, dst_ref=block,
+                send_sem=p_send.at[step, dx * rows + dr], recv_sem=p_recv.at[step, dx * rows + dr],
+                device_id={"depth": depth_at(dx), "row": row_at(dr)}, device_id_type=MESH,
+            )
+            for dx, dr in siblings
+        ]
 
     def point_copy(step):
-        to = lax.rem(me + views - step, views)
         return pltpu.make_async_remote_copy(
             src_ref=cbuf.at[me], dst_ref=cbuf.at[me],
             send_sem=i_send.at[step], recv_sem=i_recv.at[step],
-            device_id={"view": to}, device_id_type=MESH,
-        )
+            device_id={"view": paired(step)}, device_id_type=MESH,
+        )
+
+    pl.semaphore_wait(barrier, views + len(siblings) - 1)
+    for dr in range(1, rows):
+        own_copy(dr).start()
+    others(lambda step: feat_copy(step).start())
 
     for copy in local[:3]:
         copy.wait()
@@ -113,11 +128,7 @@
         cbuf[me, 0, at, :] = sbuf[d].astype(F32) + wbuf[0, d].astype(F32) / 256.0
         cbuf[me, 1, at, :] = qbuf[d].astype(F32) + wbuf[1, d].astype(F32) / 256.0
 
-    pl.semaphore_wait(barrier, views + len(siblings) - 1)
-    for dr in range(1, rows):
-        own_copy(dr).start()
-    over_views(1, lambda step: feat_copy(step).start())
-    over_views(1, lambda step: point_copy(step).start())
+    others(lambda step: point_copy(step).start())
 
     lane = lax.broadcasted_iota(jnp.int32, (SPAN, COLS), 0).astype(F32).astype(BF16)
 
@@ -180,18 +191,18 @@
 
     def pass_features(step):
         feat_copy(step).wait_recv()
-        for dr in range(1, rows):
-            pass_copy(step, dr).start()
-
-    over_views(1, pass_features)
+        for copy in pass_copies(step):
+            copy.start()
+
+    others(pass_features)
 
     def sample_step(step):
         point_copy(step).wait_recv()
-        for dr in range(1, rows):
-            pass_copy(step, dr).wait_recv()
-        sampled(view_at(step), False)
-
-    over_views(1, sample_step)
+        for copy in pass_copies(step):
+            copy.wait_recv()
+        sampled(paired(step), False)
+
+    others(sample_step)
 
     def backward(v):
         row, span, _, _ = points(v)
@@ -223,7 +234,7 @@
             for x in range(depths):
                 for i in range(rl):
                     at = (s * rl + i) * cc
-                    outbuf[v, s, x, i] = whole[at : at + cc, x * wx : (x + 1) * wx]
+                    outbuf[v, s, x, :, i, :] = whole[at : at + cc, x * wx : (x + 1) * wx]
 
     def piece_copy(v, dx, dr):
         x, r = depth_at(dx), row_at(dr)
@@ -235,50 +246,38 @@
         )
 
     def out_copy(step):
-        v = view_at(step)
-        return pltpu.make_async_remote_copy(
-            src_ref=red.at[v], dst_ref=inbuf.at[me],
+        v = paired(step)
+        return pltpu.make_async_remote_copy(
+            src_ref=red.at[v], dst_ref=out.at[pl.ds(me * cc, cc)],
             send_sem=o_send.at[step], recv_sem=o_recv.at[step],
             device_id={"view": v}, device_id_type=MESH,
         )
 
-    def add_pieces(v, target):
+    def add_pieces(v):
         piece = outbuf[v, mr, mx]
         for dx, dr in siblings:
             piece_copy(v, dx, dr).wait_recv()
             piece = piece + pbuf[v, dx * rows + dr]
-        target[...] = piece
+        return piece
 
     def pass_on(step):
-        v = view_at(step)
-        add_pieces(v, red.at[v])
+        v = paired(step)
+        red[v] = add_pieces(v)
         out_copy(step).start()
 
     def backward_step(step):
-        v = view_at(step)
+        v = paired(step)
         backward(v)
         for dx, dr in siblings:
             piece_copy(v, dx, dr).start()
-        if views <= UNROLL:
-            if step > 1:
-                pass_on(step - 1)
-        else:
-            @pl.when(step > 1)
-            def _():
-                pass_on(step - 1)
-
-    over_views(1, backward_step)
+    pl.loop(1, views)(lambda at: backward_step(views - at))
     backward(me)
     for dx, dr in siblings:
         piece_copy(me, dx, dr).start()
-    if views > 1:
-        pass_on(views - 1)
-    add_pieces(me, inbuf.at[me])
-
-    over_views(1, lambda step: out_copy(step).wait_recv())
-    for i in range(rl):
-        for u in range(views):
-            out[i, pl.ds(u * cc, cc), :] = inbuf[u, i]
+    others(pass_on)
+    out[pl.ds(me * cc, cc)] = add_pieces(me)
+
+    others(lambda step: out_copy(step).wait_recv())
 
     for dr in range(1, rows):
         own_copy(dr).wait_send()
@@ -288,13 +287,13 @@
     def finish(step):
         feat_copy(step).wait_send()
         point_copy(step).wait_send()
-        for dr in range(1, rows):
-            pass_copy(step, dr).wait_send()
+        for copy in pass_copies(step):
+            copy.wait_send()
         for dx, dr in siblings:
-            piece_copy(view_at(step), dx, dr).wait_send()
+            piece_copy(paired(step), dx, dr).wait_send()
         out_copy(step).wait_send()
 
-    over_views(1, finish)
+    others(finish)
 
 
 def per_device(features, cotangent, src_row, src_col, fractions):
@@ -307,7 +306,7 @@
     sizes = (views, depths, rows, cc, planes, rl, width)
     grad = pl.pallas_call(
         functools.partial(kernel, sizes),
-        out_shape=jax.ShapeDtypeStruct((rl, channels, wx), F32),
+        out_shape=pltpu.VMEM((channels, rl, wx), F32),
         in_specs=[pl.BlockSpec(memory_space=pl.ANY)] * 5,
         out_specs=pl.BlockSpec(memory_space=pltpu.VMEM),
         scratch_shapes=[
@@ -323,15 +322,14 @@
             pltpu.VMEM((2 * height * spans * cc, lines * width), BF16),
             pltpu.VMEM((views, lines, cc, width), F32),
             pltpu.VMEM((lines, cc, width), F32),
-            pltpu.VMEM((views, rows, depths, rl, cc, wx), F32),
-            pltpu.VMEM((views, rows * depths, rl, cc, wx), F32),
-            pltpu.VMEM((views, rl, cc, wx), F32),
-            pltpu.VMEM((views, rl, cc, wx), F32),
+            pltpu.VMEM((views, rows, depths, cc, rl, wx), F32),
+            pltpu.VMEM((views, rows * depths, cc, rl, wx), F32),
+            pltpu.VMEM((views, cc, rl, wx), F32),
             pltpu.SemaphoreType.DMA((5,)),
             pltpu.SemaphoreType.DMA((views,)),
             pltpu.SemaphoreType.DMA((views,)),
-            pltpu.SemaphoreType.DMA((views, rows)),
-            pltpu.SemaphoreType.DMA((views, rows)),
+            pltpu.SemaphoreType.DMA((views, rows * depths)),
+            pltpu.SemaphoreType.DMA((views, rows * depths)),
             pltpu.SemaphoreType.DMA((views,)),
             pltpu.SemaphoreType.DMA((views,)),
             pltpu.SemaphoreType.DMA((views, rows * depths)),
@@ -343,7 +341,7 @@
             collective_id=0, has_side_effects=True, vmem_limit_bytes=60 << 20
         ),
     )(features, cotangent, src_row, src_col, fractions)
-    return jnp.transpose(grad, (1, 0, 2))[None]
+    return grad[None]
 
 
 def solution(mesh):

time: 27.8 us -> 23.3 us (0.84)
  Pallas kernels: 26 us -> 22.5 us
  local copies, waits for them, and re-layouts: 1.52 us -> 0.63 us
    pallas_call x1, Pallas kernels: 26 us -> 22.5 us  [per_device(): pl.pallas_call(functools.partial(kernel, sizes), out_shape=pltpu.VMEM((ch...]
    broadcast_in_dim x1 -> x0, local copies, waits for them, and re-layouts: 1.52 us -> none  [per_device(): return jnp.transpose(grad, (1, 0, 2))[None]]
    unnamed x0 -> x1, local copies, waits for them, and re-layouts: none -> 0.63 us
where the time goes in v2:
time: 23.3 us; the launch traced here: 23.1 us
  Pallas kernels  22.5 us (97%)
  local copies, waits for them, and re-layouts  0.63 us (3%)
    pallas_call x1, Pallas kernels, per_device(): pl.pallas_call(functools.partial(kernel, sizes), out_shape=pltpu.VMEM((ch...  22.5 us
    unnamed x1, local copies, waits for them, and re-layouts  0.63 us

profile of v2, /device:TPU:0, one launch (start us, length us, event | category | flops | bytes accessed | tf_op | source)
XLA Modules:
  0.0 23.1 jit_solution(17536761600083819030)
XLA Ops:
  0.0 22.5 %shard_map.55 = f32[32,2,256]{2,1,0:T(2,128)S(1)} custom-call(f32[1,32,2,512]{3,2,1,0:T(2,128)} %feat.1, f32[4,8,2,512]{3,2,1,0:T(2,128)} %cot.1, s32[1,4,2,512]{3,2,1,0:T(2,128)} %srow.1, s32[1,4,2,512]{3,2,1,0:T(2,128)} %scol.1, s32[2,1,4,2,512]{4,3,2,1,0:T(2,128)} %frac.1), custom_call_target="tpu_custom_call" | custom-call | tf_op jit(solution)/shard_map/pallas_call | solution.py:307
  22.5 0.6 %copy.7 = f32[1,32,2,256]{3,2,1,0:T(2,128)} copy(f32[1,32,2,256]{3,2,1,0:T(2,128)S(1)} %bitcast.1) | data formatting | bytes 131072

commit v3 on v2

v3 whole, which is shorter than its diff:
```python
import functools

import jax
import jax.numpy as jnp
from jax import lax
from jax.experimental import pallas as pl
from jax.experimental.pallas import tpu as pltpu
from jax.sharding import PartitionSpec as P

MESH = pl.DeviceIdType.MESH
F32 = jnp.float32
BF16 = jnp.bfloat16
SPAN = 128
COLS = 256
UNROLL = 4


def split(value, axis):
    high = value.astype(BF16)
    low = (value - high.astype(F32)).astype(BF16)
    return jnp.concatenate([high, low], axis=axis)


def kernel(
    sizes, feat, cot, srow, scol, frac, out,
    fbuf, sbuf, qbuf, wbuf, cbuf, cotv, cotg, flat, edge, mats, moved, warp, wsum, outbuf, pbuf, red, inbuf,
    local_sem, f_send, f_recv, p_send, p_recv, i_send, i_recv, d_send, d_recv, o_send, o_recv,
):
    views, depths, rows, cc, planes, rl, width = sizes
    me = lax.axis_index("view")
    mx = lax.axis_index("depth")
    mr = lax.axis_index("row")
    height = rows * rl
    wx = width // depths
    lines = planes * rl
    spans = width // SPAN
    half = height * cc
    factor = 2.0 / views
    siblings = [(dx, dr) for dx in range(depths) for dr in range(rows) if dx or dr]

    def row_at(step):
        return lax.rem(mr + step, rows)

    def depth_at(step):
        return lax.rem(mx + step, depths)

    def step_of(at):
        return (views // 2 + at - 2) % (views - 1) + 1

    steps = [step_of(at) for at in range(1, views)]

    def paired(step):
        other, bit = 0, 1
        while bit < views:
            other = other + bit * lax.rem(me // bit + step // bit, 2)
            bit *= 2
        return other

    def lowest(step):
        return step & -step

    barrier = pltpu.get_barrier_semaphore()

    def greet(v, x, r):
        pl.semaphore_signal(
            barrier, inc=1, device_id={"view": v, "depth": x, "row": r}, device_id_type=MESH
        )

    for step in steps:
        greet(paired(step), mx, mr)
    for dx in range(1, depths):
        for step in steps:
            greet(paired(step), depth_at(dx), mr)
        greet(me, depth_at(dx), mr)
    for dr in range(1, rows):
        greet(me, mx, row_at(dr))

    local = [
        pltpu.make_async_copy(srow.at[0], sbuf, local_sem.at[0]),
        pltpu.make_async_copy(scol.at[0], qbuf, local_sem.at[1]),
        pltpu.make_async_copy(frac.at[:, 0], wbuf, local_sem.at[2]),
        pltpu.make_async_copy(feat.at[0, pl.ds(me * cc, cc)], fbuf.at[me, mr], local_sem.at[3]),
        pltpu.make_async_copy(cot, cotv, local_sem.at[4]),
    ]
    for copy in local:
        copy.start()

    def feat_copy(step):
        to = paired(step)
        return pltpu.make_async_remote_copy(
            src_ref=feat.at[0, pl.ds(to * cc, cc)], dst_ref=fbuf.at[me, mr],
            send_sem=f_send.at[step], recv_sem=f_recv.at[step],
            device_id={"view": to}, device_id_type=MESH,
        )

    def own_copy(dr):
        return pltpu.make_async_remote_copy(
            src_ref=feat.at[0, pl.ds(me * cc, cc)], dst_ref=fbuf.at[me, mr],
            send_sem=p_send.at[0, dr], recv_sem=p_recv.at[0, dr],
            device_id={"row": row_at(dr)}, device_id_type=MESH,
        )

    def pass_copies(step):
        block = fbuf.at[paired(step), mr]
        return [
            pltpu.make_async_remote_copy(
                src_ref=block, dst_ref=block,
                send_sem=p_send.at[step, dr], recv_sem=p_recv.at[step, dr],
                device_id={"row": row_at(dr)}, device_id_type=MESH,
            )
            for dr in range(1, rows)
        ]

    def point_copy(step):
        block = cbuf.at[paired(step - lowest(step))]
        return pltpu.make_async_remote_copy(
            src_ref=block, dst_ref=block,
            send_sem=i_send.at[step], recv_sem=i_recv.at[step],
            device_id={"view": paired(lowest(step))}, device_id_type=MESH,
        )

    for copy in local[:3]:
        copy.wait()
    for d in range(planes):
        at = pl.ds(d * rl, rl)
        cbuf[me, 0, at, :] = sbuf[d].astype(F32) + wbuf[0, d].astype(F32) / 256.0
        cbuf[me, 1, at, :] = qbuf[d].astype(F32) + wbuf[1, d].astype(F32) / 256.0

    pl.semaphore_wait(barrier, views * depths + rows - 2)
    own_points = [step for step in steps if step == lowest(step)]
    for step in own_points:
        point_copy(step).start()
    for dr in range(1, rows):
        own_copy(dr).start()
    for step in steps:
        feat_copy(step).start()

    lane = lax.broadcasted_iota(jnp.int32, (SPAN, COLS), 0).astype(F32).astype(BF16)

    def points(v):
        position = cbuf[v, 1]
        span = jnp.zeros_like(position)
        for t in range(1, spans):
            span = span + jnp.where(position >= float(t * SPAN), 1.0, 0.0)
        inside = position - span * float(SPAN)
        whole = jnp.floor(inside)
        rest = inside - whole
        return cbuf[v, 0], span, whole, rest, jnp.where(whole == float(SPAN - 1), rest, 0.0)

    def row_weight(row, k, h):
        return jnp.maximum(1.0 - jnp.abs(row[k : k + 1] - float(h)), 0.0)

    def flatten(v):
        parts = []
        for h in range(height):
            line = fbuf[v, h // rl, :, h % rl, :]
            for t in range(spans):
                parts.append(line[:, t * SPAN : (t + 1) * SPAN])
                if t:
                    first = line[:, t * SPAN : t * SPAN + 1]
                    edge[h, t - 1] = jnp.broadcast_to(first, (cc, COLS))
        flat[...] = split(jnp.concatenate(parts, axis=0), 1)

    def sampled(v, first):
        flatten(v)
        row, span, whole, rest, over = points(v)
        for k in range(lines):
            for n in range(0, width, COLS):
                cols = slice(n, n + COLS)
                at = jnp.broadcast_to(whole[k : k + 1, cols].astype(BF16), (SPAN, COLS))
                past = jnp.broadcast_to(rest[k : k + 1, cols].astype(BF16), (SPAN, COLS))
                mat = jnp.maximum(BF16(1.0) - jnp.abs((lane - at) - past), BF16(0.0))
                mats[v, :, k * width + n : k * width + n + COLS] = mat
                mixed = jnp.dot(
                    flat[...], jnp.concatenate([mat, mat], axis=0), preferred_element_type=F32
                )
                which = jnp.broadcast_to(span[k : k + 1, cols], (cc, COLS))
                beyond = jnp.broadcast_to(over[k : k + 1, cols], (cc, COLS))
                warped = None
                for h in range(height):
                    base = h * spans * cc
                    part, tail = mixed[base : base + cc], edge[h, 0] if spans > 1 else None
                    for t in range(1, spans):
                        here = base + t * cc
                        inside = which == float(t)
                        part = jnp.where(inside, mixed[here : here + cc], part)
                        if t < spans - 1:
                            tail = jnp.where(inside, edge[h, t], tail)
                    if tail is not None:
                        part = part + beyond * tail
                    part = part * row_weight(row, k, h)[:, cols]
                    warped = part if warped is None else warped + part
                warp[v, k, :, cols] = warped
                wsum[k, :, cols] = warped if first else wsum[k, :, cols] + warped

    local[4].wait()
    for k in range(lines):
        cotg[k] = factor * cotv[k // rl, :, k % rl, :]
    local[3].wait()
    for dr in range(1, rows):
        own_copy(dr).wait_recv()
    sampled(me, True)

    bit = views // 4
    while bit:
        for step in steps:
            if lowest(step) == 2 * bit:
                point_copy(step).wait_recv()
        for step in steps:
            if lowest(step) == bit and step != bit:
                point_copy(step).start()
        bit //= 2

    for step in sorted(steps):
        feat_copy(step).wait_recv()
        for copy in pass_copies(step):
            copy.start()

    def ready(step):
        if lowest(step) == 1:
            point_copy(step).wait_recv()
        for copy in pass_copies(step):
            copy.wait_recv()

    if views <= UNROLL:
        for step in sorted(steps):
            ready(step)
            sampled(paired(step), False)
    else:
        for step in steps:
            ready(step)
        pl.loop(1, views)(lambda step: sampled(paired(step), False))

    def backward(v):
        row, span, _, _, over = points(v)
        size = 2 * half
        crossing = [jnp.zeros((half, SPAN), F32)] * (spans - 1)
        for k in range(lines):
            grad = cotg[k] * (warp[v, k] - wsum[k] / views)
            spread = jnp.concatenate([grad * row_weight(row, k, h) for h in range(height)], axis=0)
            both = split(spread, 0)
            for t in range(spans):
                mask = jnp.where(span[k : k + 1] == float(t), 1.0, 0.0)
                moved[t * size : (t + 1) * size, k * width : (k + 1) * width] = both * mask.astype(BF16)
                if t < spans - 1:
                    beyond = spread * (mask * over[k : k + 1])
                    for n in range(0, width, SPAN):
                        crossing[t] = crossing[t] + beyond[:, n : n + SPAN]
        total = lax.dot_general(
            moved[...], mats[v], (((1,), (1,)), ((), ())), preferred_element_type=F32
        )
        starts = lax.broadcasted_iota(jnp.int32, (half, SPAN), 1) == 0
        for t in range(spans):
            part = total[t * size : t * size + half] + total[t * size + half : (t + 1) * size]
            if t:
                part = part + jnp.where(starts, jnp.sum(crossing[t - 1], axis=1, keepdims=True), 0.0)
            x, left = t * SPAN // wx, t * SPAN % wx
            for s in range(rows):
                for i in range(rl):
                    at = (s * rl + i) * cc
                    outbuf[v, s, x, :, i, left : left + SPAN] = part[at : at + cc]

    def core_copy(v, dr):
        r = row_at(dr)
        return pltpu.make_async_remote_copy(
            src_ref=outbuf.at[v, r], dst_ref=pbuf.at[v, dr],
            send_sem=d_send.at[v, dr], recv_sem=d_recv.at[v, dr],
            device_id={"row": r}, device_id_type=MESH,
        )

    def out_copy(v, step, dx):
        x = depth_at(dx)
        return pltpu.make_async_remote_copy(
            src_ref=red.at[v, x], dst_ref=inbuf.at[me, mx],
            send_sem=o_send.at[step, dx], recv_sem=o_recv.at[step, dx],
            device_id={"view": v, "depth": x}, device_id_type=MESH,
        )

    def add_cores(v):
        piece = outbuf[v, mr]
        for dr in range(1, rows):
            core_copy(v, dr).wait_recv()
            piece = piece + pbuf[v, dr]
        red[v] = piece

    def other_at(at):
        return at - 1 + (at - 1 + views - me) // views

    def pass_on(v):
        add_cores(v)
        for dx in range(depths):
            out_copy(v, paired(v), dx).start()

    @pl.loop(1, views)
    def _(at):
        v = other_at(at)
        backward(v)
        for dr in range(1, rows):
            core_copy(v, dr).start()

        @pl.when(at > 1)
        def _():
            pass_on(other_at(at - 1))

    backward(me)
    for dr in range(1, rows):
        core_copy(me, dr).start()
    if views > 1:
        pass_on(other_at(views - 1))
    add_cores(me)
    for dx in range(1, depths):
        out_copy(me, 0, dx).start()
    inbuf[me, mx] = red[me, mx]

    def arrived(step):
        for dx in range(depths):
            out_copy(paired(step), step, dx).wait_recv()

    for step in steps:
        arrived(step)
    for dx in range(1, depths):
        out_copy(me, 0, dx).wait_recv()
    for u in range(views):
        piece = inbuf[u, 0]
        for x in range(1, depths):
            piece = piece + inbuf[u, x]
        out[u * cc : (u + 1) * cc] = piece

    for dr in range(1, rows):
        own_copy(dr).wait_send()
        core_copy(me, dr).wait_send()
    for dx in range(1, depths):
        out_copy(me, 0, dx).wait_send()

    def finish(step):
        feat_copy(step).wait_send()
        point_copy(step).wait_send()
        for copy in pass_copies(step):
            copy.wait_send()
        for dr in range(1, rows):
            core_copy(paired(step), dr).wait_send()
        for dx in range(depths):
            out_copy(paired(step), step, dx).wait_send()

    for step in steps:
        finish(step)


def per_device(features, cotangent, src_row, src_col, fractions):
    views, depths, rows = (lax.axis_size(axis) for axis in ("view", "depth", "row"))
    channels, rl, width = features.shape[1:]
    planes, cc = cotangent.shape[:2]
    height, wx = rows * rl, width // depths
    lines = planes * rl
    spans = width // SPAN
    sizes = (views, depths, rows, cc, planes, rl, width)
    grad = pl.pallas_call(
        functools.partial(kernel, sizes),
        out_shape=pltpu.VMEM((channels, rl, wx), F32),
        in_specs=[pl.BlockSpec(memory_space=pl.ANY)] * 5,
        out_specs=pl.BlockSpec(memory_space=pltpu.VMEM),
        scratch_shapes=[
            pltpu.VMEM((views, rows, cc, rl, width), F32),
            pltpu.VMEM((planes, rl, width), jnp.int32),
            pltpu.VMEM((planes, rl, width), jnp.int32),
            pltpu.VMEM((2, planes, rl, width), jnp.int32),
            pltpu.VMEM((views, 2, lines, width), F32),
            pltpu.VMEM((planes, cc, rl, width), F32),
            pltpu.VMEM((lines, cc, width), F32),
            pltpu.VMEM((height * spans * cc, 2 * SPAN), BF16),
            pltpu.VMEM((height, max(spans - 1, 1), cc, COLS), F32),
            pltpu.VMEM((views, SPAN, lines * width), BF16),
            pltpu.VMEM((2 * height * spans * cc, lines * width), BF16),
            pltpu.VMEM((views, lines, cc, width), F32),
            pltpu.VMEM((lines, cc, width), F32),
            pltpu.VMEM((views, rows, depths, cc, rl, wx), F32),
            pltpu.VMEM((views, rows, depths, cc, rl, wx), F32),
            pltpu.VMEM((views, depths, cc, rl, wx), F32),
            pltpu.VMEM((views, depths, cc, rl, wx), F32),
            pltpu.SemaphoreType.DMA((5,)),
            pltpu.SemaphoreType.DMA((views,)),
            pltpu.SemaphoreType.DMA((views,)),
            pltpu.SemaphoreType.DMA((views, rows)),
            pltpu.SemaphoreType.DMA((views, rows)),
            pltpu.SemaphoreType.DMA((views,)),
            pltpu.SemaphoreType.DMA((views,)),
            pltpu.SemaphoreType.DMA((views, rows)),
            pltpu.SemaphoreType.DMA((views, rows)),
            pltpu.SemaphoreType.DMA((views, depths)),
            pltpu.SemaphoreType.DMA((views, depths)),
        ],
        compiler_params=pltpu.CompilerParams(
            collective_id=0, has_side_effects=True, vmem_limit_bytes=60 << 20
        ),
    )(features, cotangent, src_row, src_col, fractions)
    return grad[None]


def solution(mesh):
    in_specs = (
        P("view", None, ("group", "row"), None),
        P("depth", "view", ("group", "row"), None),
        P("view", "depth", ("group", "row"), None),
        P("view", "depth", ("group", "row"), None),
        P(None, "view", "depth", ("group", "row"), None),
    )
    out_specs = P("view", None, ("group", "row"), "depth")
    return jax.shard_map(
        per_device, mesh=mesh, in_specs=in_specs, out_specs=out_specs, check_vma=False
    )
```

time: 23.3 us -> 22.1 us (0.948)
  Pallas kernels: 22.5 us -> 21.2 us
    pallas_call x1, Pallas kernels: 22.5 us -> 21.2 us  [per_device(): pl.pallas_call(functools.partial(kernel, sizes), out_shape=pltpu.VMEM((ch...]
where the time goes in v3:
time: 22.1 us; the launch traced here: 21.8 us
  Pallas kernels  21.2 us (96%)
  local copies, waits for them, and re-layouts  0.63 us (3%)
    pallas_call x1, Pallas kernels, per_device(): pl.pallas_call(functools.partial(kernel, sizes), out_shape=pltpu.VMEM((ch...  21.2 us
    unnamed x1, local copies, waits for them, and re-layouts  0.63 us

profile of v3, /device:TPU:0, one launch (start us, length us, event | category | flops | bytes accessed | tf_op | source)
XLA Modules:
  0.0 21.8 jit_solution(6114931456019282397)
XLA Ops:
  0.0 21.2 %shard_map.55 = f32[32,2,256]{2,1,0:T(2,128)S(1)} custom-call(f32[1,32,2,512]{3,2,1,0:T(2,128)} %feat.1, f32[4,8,2,512]{3,2,1,0:T(2,128)} %cot.1, s32[1,4,2,512]{3,2,1,0:T(2,128)} %srow.1, s32[1,4,2,512]{3,2,1,0:T(2,128)} %scol.1, s32[2,1,4,2,512]{4,3,2,1,0:T(2,128)} %frac.1), custom_call_target="tpu_custom_call" | custom-call | tf_op jit(solution)/shard_map/pallas_call | solution.py:357
  21.2 0.6 %copy.7 = f32[1,32,2,256]{3,2,1,0:T(2,128)} copy(f32[1,32,2,256]{3,2,1,0:T(2,128)S(1)} %bitcast.1) | data formatting | bytes 131072

commit v4 on v3

--- a/solution.py
+++ b/solution.py
@@ -45,7 +45,7 @@
         return lax.rem(mx + step, depths)
 
     def step_of(at):
-        return (views // 2 + at - 2) % (views - 1) + 1
+        return views - at
 
     steps = [step_of(at) for at in range(1, views)]
 
@@ -132,7 +132,7 @@
         point_copy(step).start()
     for dr in range(1, rows):
         own_copy(dr).start()
-    for step in steps:
+    for step in range(1, views):
         feat_copy(step).start()
 
     lane = lax.broadcasted_iota(jnp.int32, (SPAN, COLS), 0).astype(F32).astype(BF16)
@@ -211,7 +211,7 @@
                 point_copy(step).start()
         bit //= 2
 
-    for step in sorted(steps):
+    def hand_on(step):
         feat_copy(step).wait_recv()
         for copy in pass_copies(step):
             copy.start()
@@ -222,12 +222,19 @@
         for copy in pass_copies(step):
             copy.wait_recv()
 
+    def sample(step):
+        ready(step)
+        sampled(paired(step), False)
+
     if views <= UNROLL:
-        for step in sorted(steps):
-            ready(step)
-            sampled(paired(step), False)
+        for step in range(1, views):
+            hand_on(step)
+        for step in range(1, views):
+            sample(step)
     else:
-        for step in steps:
+        for step in range(1, views):
+            hand_on(step)
+        for step in range(1, views):
             ready(step)
         pl.loop(1, views)(lambda step: sampled(paired(step), False))
 

time: 22.1 us -> 21.5 us (0.973)
  Pallas kernels: 21.2 us -> 20.7 us
    pallas_call x1, Pallas kernels: 21.2 us -> 20.7 us  [per_device(): pl.pallas_call(functools.partial(kernel, sizes), out_shape=pltpu.VMEM((ch...]
where the time goes in v4:
time: 21.5 us; the launch traced here: 21.3 us
  Pallas kernels  20.7 us (96%)
  local copies, waits for them, and re-layouts  0.63 us (3%)
    pallas_call x1, Pallas kernels, per_device(): pl.pallas_call(functools.partial(kernel, sizes), out_shape=pltpu.VMEM((ch...  20.7 us
    unnamed x1, local copies, waits for them, and re-layouts  0.63 us

profile of v4, /device:TPU:0, one launch (start us, length us, event | category | flops | bytes accessed | tf_op | source)
XLA Modules:
  0.0 21.3 jit_solution(18061351012319912880)
XLA Ops:
  0.0 20.7 %shard_map.55 = f32[32,2,256]{2,1,0:T(2,128)S(1)} custom-call(f32[1,32,2,512]{3,2,1,0:T(2,128)} %feat.1, f32[4,8,2,512]{3,2,1,0:T(2,128)} %cot.1, s32[1,4,2,512]{3,2,1,0:T(2,128)} %srow.1, s32[1,4,2,512]{3,2,1,0:T(2,128)} %scol.1, s32[2,1,4,2,512]{4,3,2,1,0:T(2,128)} %frac.1), custom_call_target="tpu_custom_call" | custom-call | tf_op jit(solution)/shard_map/pallas_call | solution.py:364
  20.7 0.6 %copy.7 = f32[1,32,2,256]{3,2,1,0:T(2,128)} copy(f32[1,32,2,256]{3,2,1,0:T(2,128)S(1)} %bitcast.1) | data formatting | bytes 131072

commit v5 on v4

--- a/solution.py
+++ b/solution.py
@@ -290,33 +290,31 @@
             piece = piece + pbuf[v, dr]
         red[v] = piece
 
-    def other_at(at):
-        return at - 1 + (at - 1 + views - me) // views
-
     def pass_on(v):
         add_cores(v)
-        for dx in range(depths):
+        for dx in range(1, depths):
             out_copy(v, paired(v), dx).start()
 
-    @pl.loop(1, views)
+        @pl.when(v != me)
+        def _():
+            out_copy(v, paired(v), 0).start()
+
+    def view_at(at):
+        return lax.rem(at + (views - me) // views * (views - at - at), views)
+
+    @pl.loop(0, views + 1)
     def _(at):
-        v = other_at(at)
-        backward(v)
-        for dr in range(1, rows):
-            core_copy(v, dr).start()
-
-        @pl.when(at > 1)
+        @pl.when(at < views)
         def _():
-            pass_on(other_at(at - 1))
-
-    backward(me)
-    for dr in range(1, rows):
-        core_copy(me, dr).start()
-    if views > 1:
-        pass_on(other_at(views - 1))
-    add_cores(me)
-    for dx in range(1, depths):
-        out_copy(me, 0, dx).start()
+            v = view_at(at)
+            backward(v)
+            for dr in range(1, rows):
+                core_copy(v, dr).start()
+
+        @pl.when(at > 0)
+        def _():
+            pass_on(view_at(at - 1))
+
     inbuf[me, mx] = red[me, mx]
 
     def arrived(step):

time: 21.5 us -> 21.3 us (level)
  no operation moved by 1% of the time
where the time goes in v5:
time: 21.3 us; the launch traced here: 21.1 us
  Pallas kernels  20.5 us (96%)
  local copies, waits for them, and re-layouts  0.63 us (3%)
    pallas_call x1, Pallas kernels, per_device(): pl.pallas_call(functools.partial(kernel, sizes), out_shape=pltpu.VMEM((ch...  20.5 us
    unnamed x1, local copies, waits for them, and re-layouts  0.63 us

profile of v5, /device:TPU:0, one launch (start us, length us, event | category | flops | bytes accessed | tf_op | source)
XLA Modules:
  0.0 21.1 jit_solution(10757896502958723895)
XLA Ops:
  0.0 20.5 %shard_map.55 = f32[32,2,256]{2,1,0:T(2,128)S(1)} custom-call(f32[1,32,2,512]{3,2,1,0:T(2,128)} %feat.1, f32[4,8,2,512]{3,2,1,0:T(2,128)} %cot.1, s32[1,4,2,512]{3,2,1,0:T(2,128)} %srow.1, s32[1,4,2,512]{3,2,1,0:T(2,128)} %scol.1, s32[2,1,4,2,512]{4,3,2,1,0:T(2,128)} %frac.1), custom_call_target="tpu_custom_call" | custom-call | tf_op jit(solution)/shard_map/pallas_call | solution.py:362
  20.5 0.6 %copy.7 = f32[1,32,2,256]{3,2,1,0:T(2,128)} copy(f32[1,32,2,256]{3,2,1,0:T(2,128)S(1)} %bitcast.1) | data formatting | bytes 131072

commit v6 on v5

--- a/solution.py
+++ b/solution.py
@@ -193,9 +193,6 @@
                 warp[v, k, :, cols] = warped
                 wsum[k, :, cols] = warped if first else wsum[k, :, cols] + warped
 
-    local[4].wait()
-    for k in range(lines):
-        cotg[k] = factor * cotv[k // rl, :, k % rl, :]
     local[3].wait()
     for dr in range(1, rows):
         own_copy(dr).wait_recv()
@@ -226,6 +223,9 @@
         ready(step)
         sampled(paired(step), False)
 
+    local[4].wait()
+    for k in range(lines):
+        cotg[k] = factor * cotv[k // rl, :, k % rl, :]
     if views <= UNROLL:
         for step in range(1, views):
             hand_on(step)

time: 21.3 us -> 21.3 us (level)
  no operation moved by 1% of the time
where the time goes in v6:
time: 21.3 us; the launch traced here: 21.1 us
  Pallas kernels  20.5 us (96%)
  local copies, waits for them, and re-layouts  0.63 us (3%)
    pallas_call x1, Pallas kernels, per_device(): pl.pallas_call(functools.partial(kernel, sizes), out_shape=pltpu.VMEM((ch...  20.5 us
    unnamed x1, local copies, waits for them, and re-layouts  0.63 us

profile of v6, /device:TPU:0, one launch (start us, length us, event | category | flops | bytes accessed | tf_op | source)
XLA Modules:
  0.0 21.1 jit_solution(260861927241702236)
XLA Ops:
  0.0 20.5 %shard_map.55 = f32[32,2,256]{2,1,0:T(2,128)S(1)} custom-call(f32[1,32,2,512]{3,2,1,0:T(2,128)} %feat.1, f32[4,8,2,512]{3,2,1,0:T(2,128)} %cot.1, s32[1,4,2,512]{3,2,1,0:T(2,128)} %srow.1, s32[1,4,2,512]{3,2,1,0:T(2,128)} %scol.1, s32[2,1,4,2,512]{4,3,2,1,0:T(2,128)} %frac.1), custom_call_target="tpu_custom_call" | custom-call | tf_op jit(solution)/shard_map/pallas_call | solution.py:362
  20.5 0.6 %copy.7 = f32[1,32,2,256]{3,2,1,0:T(2,128)} copy(f32[1,32,2,256]{3,2,1,0:T(2,128)S(1)} %bitcast.1) | data formatting | bytes 131072
